TPU v7x, 256 devices: a whole 4x4x8 slice. The times are simulated.
256 devices in a mesh: expert: 32 (over z_hi, y, core), dp: 8 (over z_lo, x).
Axes of the slice: x: 4, y: 4, z: 8 (z_hi: 4, z_lo: 2; z = z_hi * 2 + z_lo), core: 2. Of those that a mesh axis runs over, the one named last changes fastest.
Arguments:
- tokens: bfloat16 [32768, 4096], P(('expert', 'dp')), may hold values from -6 to 6
- route: int32 [32768, 2], P(('expert', 'dp')), may hold values from 0 to 63, all different within a row; in each aligned block of 128 rows (0 to 127, 128 to 255, ...) at most 12 rows name the same one
- gate_output_gradient: bfloat16 [32768, 2, 1536], P(('expert', 'dp')), may hold values from -0.4375 to 0.4375
- frozen_gate_weight: bfloat16 [64, 4096, 1536], P('expert', 'dp'), may hold values from -0.09375 to 0.09375
- adapter_first: bfloat16 [64, 4096, 16], P('expert'), may hold values from -0.09375 to 0.09375
- adapter_second: bfloat16 [64, 16, 1536], P('expert'), may hold values from -0.15625 to 0.15625
Outputs:
- grad_a: float32 [64, 4096, 16], P('expert')
- grad_b: float32 [64, 16, 1536], P('expert')
Inputs may be any that keep to these rules, and one draw needn't show every extreme that they name: `route`: each row names 2 different experts. Within each device's aligned block of 128 rows no expert is named more than 12 times.
All inputs are finite; a program needn't handle non-finite values.
Results may differ from a plain program's by a relative error of at most 0.0043.
Values may be sent and summed in bfloat16 or wider, within the bound.
No kernel may reach another device: no remote copies, remote signals or barrier semaphores. Data moves between devices by JAX's collectives and lax.ppermute only.
A program may use at most 128 MiB of HBM per device.

v0:
```python
import jax
import jax.numpy as jnp
from jax import lax
from jax.sharding import Mesh, PartitionSpec as P

ADAPTER_SCALE = 2.0
EXPERT_AXES = ("zh", "y", "c")
DP_AXES = ("zl", "x")
PLANE = ("zh", "y", "c", "zl")


def dot(a, b, dims=((1,), (0,))):
    return lax.dot_general(a, b, (dims, ((), ())), preferred_element_type=jnp.float32)


def silu_slope(gate_preactivation):
    squash = jax.nn.sigmoid(gate_preactivation)
    return squash * (1.0 + gate_preactivation * (1.0 - squash))


def slot_targets(route, cap):
    rows, top = route.shape
    flat = route.T.reshape(rows * top)
    before = jnp.arange(rows * top)[:, None] > jnp.arange(rows * top)[None, :]
    same = flat[:, None] == flat[None, :]
    ranks = jnp.sum((same & before).astype(jnp.int32), axis=1)
    return (flat * cap + ranks).reshape(top, rows)


def send_places(experts, cap, swap):
    p = jnp.arange(experts * 24, dtype=jnp.int32)
    e, piece, r = (p // 24, p % 24 // 8, p % 8)
    rank = jnp.where(piece < 2, r, 8 + r % 4)
    half = jnp.where(piece < 2, piece, r // 4)
    if swap:
        half = jnp.where(e % 2 == 1, 1 - half, half)
    return (e * cap + rank, half)


def local(tokens, route, gate_output_gradient, frozen_gate_weight, adapter_first, adapter_second):
    tok_rows, width = tokens.shape
    hidden = gate_output_gradient.shape[2]
    experts = 64
    cap = 12
    zl = lax.axis_index("zl")
    mine = lax.dynamic_index_in_dim(frozen_gate_weight, zl, 0, keepdims=False)
    other = lax.dynamic_index_in_dim(frozen_gate_weight, 1 - zl, 0, keepdims=False)
    weight_near = lax.all_gather(mine, "x", axis=0, tiled=True)
    got = lax.ppermute(other, "zl", [(0, 1), (1, 0)])
    weight_far = lax.all_gather(got, "x", axis=0, tiled=True)
    first = lax.dynamic_index_in_dim(adapter_first, zl, 0, keepdims=False)
    second = lax.dynamic_index_in_dim(adapter_second, zl, 0, keepdims=False)
    half_width = width // 2
    first = jnp.where(zl == 0, first, jnp.roll(first, half_width, axis=0))
    target = slot_targets(route, cap)
    place, half = send_places(experts, cap, True)
    match = (place[:, None] == target[0][None, :]) | (place[:, None] == target[1][None, :])
    pick = jnp.concatenate([match & (half == 0)[:, None], match & (half == 1)[:, None]], axis=1)
    stack = jnp.concatenate([tokens[:, :half_width], tokens[:, half_width:]], axis=0)
    send_x = dot(pick.astype(jnp.bfloat16), stack).astype(jnp.bfloat16)
    send_x = send_x.reshape(experts, 24, half_width)
    recv_x = lax.all_to_all(send_x, PLANE, split_axis=0, concat_axis=0, tiled=True)
    place, half = send_places(experts, cap, False)
    match = place[:, None] == target.reshape(1, 2 * tok_rows)
    pick = jnp.concatenate([match & (half == 0)[:, None], match & (half == 1)[:, None]], axis=1)
    half_hidden = hidden // 2
    parts = [
        gate_output_gradient[:, k, h * half_hidden : (h + 1) * half_hidden]
        for h in range(2)
        for k in range(2)
    ]
    send_g = dot(pick.astype(jnp.bfloat16), jnp.concatenate(parts, axis=0)).astype(jnp.bfloat16)
    send_g = send_g.reshape(experts, 24, half_hidden)
    recv_g = lax.all_to_all(send_g, PLANE, split_axis=0, concat_axis=0, tiled=True)
    row = jnp.arange(4 * experts)
    col = jnp.arange(8 * experts)
    same_source = (row // 4)[:, None] == (col // 8)[None, :]

    def gather_half(received, h):
        main = received[:, 8 * h : 8 * h + 8].reshape(8 * experts, -1)
        tail = received[:, 16:24].reshape(8 * experts, -1)
        pick = same_source & ((4 * h + row % 4)[:, None] == (col % 8)[None, :])
        tail = dot(pick.astype(jnp.bfloat16), tail).astype(jnp.bfloat16)
        return jnp.concatenate([main, tail], axis=0)

    x_near = gather_half(recv_x, 0)
    x_far = gather_half(recv_x, 1)
    low = (dot(x_near, first[:half_width]) + dot(x_far, first[half_width:])).astype(jnp.bfloat16)
    frozen = dot(x_near, weight_near) + dot(x_far, weight_far)
    preact = frozen + ADAPTER_SCALE * dot(low, second)
    rows_g = jnp.concatenate([gather_half(recv_g, 0), gather_half(recv_g, 1)], axis=1)
    slope = (rows_g.astype(jnp.float32) * silu_slope(preact)).astype(jnp.bfloat16)
    back = dot(slope, second, ((1,), (1,))).astype(jnp.bfloat16)
    grads = ADAPTER_SCALE * jnp.concatenate(
        [
            dot(back, x_near, ((0,), (0,))),
            dot(back, x_far, ((0,), (0,))),
            dot(low, slope, ((0,), (0,))),
        ],
        axis=1,
    )
    rank = grads.shape[0]
    chunk = grads.shape[1] // 4
    parts = grads.reshape(rank, 4, chunk).transpose(1, 0, 2)
    parts = lax.all_to_all(parts, "x", split_axis=0, concat_axis=0, tiled=True)
    total = jnp.sum(parts, axis=0).astype(jnp.bfloat16)
    total = jnp.broadcast_to(total[None], (8, rank, chunk))
    total = lax.all_to_all(total, DP_AXES, split_axis=0, concat_axis=0, tiled=True)
    total = total.reshape(2, 4, rank, chunk).transpose(0, 2, 1, 3).reshape(2, rank, 4 * chunk)
    near, far = (total[:, :, :half_width], total[:, :, half_width:width])
    grad_a = jnp.stack(
        [jnp.concatenate([near[0], far[0]], axis=1), jnp.concatenate([far[1], near[1]], axis=1)]
    )
    grad_a = grad_a.transpose(0, 2, 1).astype(jnp.float32)
    return (grad_a, total[:, :, width:].astype(jnp.float32))


def solution(mesh):
    fine = Mesh(mesh.devices.reshape(4, 4, 2, 2, 4), EXPERT_AXES + DP_AXES)
    everyone = EXPERT_AXES + DP_AXES
    return jax.shard_map(
        local,
        mesh=fine,
        in_specs=(
            P(everyone, None),
            P(everyone, None),
            P(everyone, None, None),
            P(EXPERT_AXES, DP_AXES, None),
            P(EXPERT_AXES, None, None),
            P(EXPERT_AXES, None, None),
        ),
        out_specs=(P(EXPERT_AXES, None, None), P(EXPERT_AXES, None, None)),
        check_vma=False,
    )
```

profile of v0, /device:TPU:8, one launch (start us, length us, event | category | flops | bytes accessed | tf_op | source)
XLA Modules:
  0.0 375.5 jit_solution(1847218579089179131)
XLA Ops:
  7.2 0.9 convert_reduce_fusion
  8.2 0.7 multiply_add_fusion
  8.9 2.8 fusion.96
  11.7 1.4 compare_and_fusion.1
  13.2 2.9 convolution_convert_fusion.1
  16.0 12.1 %all-to-all-start = ((bf16[64,24,768]{2,1,0:T(8,128)(2,1)}), bf16[64,24,768]{2,1,0:T(8,128)(2,1)S(1)}, u32[]{:S(2)}, u32[]{:S(2)}) async-start(bf16[64,24,768]{2,1,0:T(8,128)(2,1)} %bitcast.80), calls=%async_computation | async-start | bytes 4718592 | tf_op jit(solution)/shard_map/all_to_all | solution.py:74
  28.2 3.9 %dynamic-slice_bitcast_fusion = (bf16[512,1536]{1,0:T(8,128)(2,1)}, bf16[1,512,1536]{2,1,0:T(8,128)(2,1)}) fusion(bf16[2,512,1536]{2,1,0:T(8,128)(2,1)} %param.9, s32[]{:T(128)S(6)} %select_n.335, s32[]{:T(128)S(6)} %select_n.334), kind=kLoop, calls=%fused_computation.17 | loop fusion | bytes 6291464 | tf_op jit(solution)/shard_map/jit(dynamic_index_in_dim)/squeeze | solution.py:47
  32.2 1.4 fusion.23
  33.7 4.5 %convolution_convert_fusion = bf16[1536,2048]{1,0:T(8,128)(2,1)} fusion(pred[1536,128]{1,0:T(32,128)(4,1)S(1)} %get-tuple-element.23, pred[1536,128]{1,0:T(32,128)(4,1)S(1)} %get-tuple-element.22, bf16[128,2048]{1,0:T(8,128)(2,1)S(1)} %get-tuple-element.9, bf16[128,2048]{1,0:T(8,128)(2,1)S(1)} %get-tuple-element.8), kind=kOutput, calls=%fused_computation | convolution fusion | flops 1616248832 | bytes 7733248 | tf_op jit(solution)/shard_map/dot_general | solution.py:13
  38.1 46.8 %all-to-all-done = bf16[64,24,768]{2,1,0:T(8,128)(2,1)S(1)} async-done(((bf16[64,24,768]{2,1,0:T(8,128)(2,1)}), bf16[64,24,768]{2,1,0:T(8,128)(2,1)S(1)}, u32[]{:S(2)}, u32[]{:S(2)}) %all-to-all-start) | async-done | bytes 2359328 | tf_op jit(solution)/shard_map/all_to_all | solution.py:74
  84.9 5.8 %all-to-all-start.1 = ((bf16[64,24,2048]{2,1,0:T(8,128)(2,1)}), bf16[64,24,2048]{2,1,0:T(8,128)(2,1)}, u32[]{:S(2)}, u32[]{:S(2)}) async-start(bf16[64,24,2048]{2,1,0:T(8,128)(2,1)} %bitcast.79), calls=%async_computation.1 | async-start | bytes 12582912 | tf_op jit(solution)/shard_map/all_to_all | solution.py:62
  90.8 1.7 collective-permute-start
  92.5 169.0 %collective-permute-done = bf16[512,1536]{1,0:T(8,128)(2,1)} collective-permute-done((bf16[512,1536]{1,0:T(8,128)(2,1)}, bf16[512,1536]{1,0:T(8,128)(2,1)}, u32[]{:S(2)}, u32[]{:S(2)}) %collective-permute-start) | collective-permute-done | bytes 1572896 | tf_op jit(solution)/shard_map/ppermute | solution.py:49
  261.6 1.2 convolution_convert_fusion.5
  262.8 1.2 convolution_convert_fusion.4
  264.0 1.1 slice_bitcast_fusion.7
  265.1 2.4 convolution_convert_fusion.3
  267.4 3.0 slice_bitcast_fusion
  270.5 0.9 fusion.14
  271.4 2.4 convolution_convert_fusion.2
  273.8 0.9 fusion.8
  274.8 2.9 fusion.44
  277.7 9.7 %fusion = f32[768,1536]{1,0:T(8,128)} fusion(bf16[1,2048,1536]{2,1,0:T(8,128)(2,1)} %all-gather.6.cloned.1.call-done, bf16[256,2048]{1,0:T(8,128)(2,1)} %copy-done.5, bf16[512,2048]{1,0:T(8,128)(2,1)} %copy-done.1), kind=kOutput, calls=%fused_computation.1 | convolution fusion | flops 4838129664 | bytes 14155776 | tf_op jit(solution)/shard_map/dot_general | solution.py:13
  287.4 42.7 %all-gather.4.cloned.1.call-done = bf16[2048,1536]{1,0:T(8,128)(2,1)} async-done(((bf16[512,1536]{1,0:T(8,128)(2,1)}), bf16[2048,1536]{1,0:T(8,128)(2,1)}) %all-gather.4.cloned.1.call-update) | async-done | bytes 6291472 | tf_op jit(solution)/shard_map/all_gather | solution.py:50
  330.1 12.5 %multiply_convert_fusion = bf16[768,1536]{1,0:T(8,128)(2,1)S(1)} fusion(f32[768,1536]{1,0:T(8,128)} %fusion.44, f32[768,1536]{1,0:T(8,128)} %fusion, bf16[2048,1536]{1,0:T(8,128)(2,1)} %all-gather.4.cloned.1.call-done, bf16[256,768]{1,0:T(8,128)(2,1)} %convolution_convert_fusion.4, bf16[512,768]{1,0:T(8,128)(2,1)} %get-tuple-element.7, ...), kind=kOutput, calls=%fused_computation.3 | convolution fusion | flops 4861722624 | bytes 23592960 | tf_op jit(solution)/shard_map/dot_general | solution.py:13
  342.6 0.7 convolution_convert_fusion.6
  343.3 0.6 fusion.13
  343.9 0.5 fusion.12
  344.9 11.0 %all_to_all.20 = f32[4,16,1408]{2,1,0:T(8,128)S(1)} all-to-all(f32[4,16,1408]{2,1,0:T(8,128)S(1)} %bitcast.84), channel_id=1, replica_groups=mesh['zh'=4,'y'=4,'c'=2,'zl'=2,'x'=4] {'x'}, dimensions={0} | all-to-all | bytes 720896 | tf_op jit(solution)/shard_map/all_to_all | solution.py:105
  356.0 11.1 %all_to_all.21 = bf16[8,16,1408]{2,1,0:T(8,128)(2,1)S(1)} all-to-all(bf16[8,16,1408]{2,1,0:T(8,128)(2,1)S(1)} %broadcast_in_dim.2), channel_id=1, replica_groups=mesh['zh'=4,'y'=4,'c'=2,'zl'=2,'x'=4] {'zl','x'}, dimensions={0} | all-to-all | bytes 720896 | tf_op jit(solution)/shard_map/all_to_all | solution.py:108
  367.1 0.7 slice_convert_fusion
  367.8 0.8 convert_bitcast_fusion
  (45 shorter events, 1.1 us)
Async XLA Ops:
  7.2 267.6 %copy-start = (bf16[2,16,1536]{2,1,0:T(8,128)(2,1)S(1)}, bf16[2,16,1536]{2,1,0:T(8,128)(2,1)}, u32[]{:S(2)}) copy-start(bf16[2,16,1536]{2,1,0:T(8,128)(2,1)} %param.11) | copy-start | bytes 294916
  16.0 68.9 %all-to-all-start = ((bf16[64,24,768]{2,1,0:T(8,128)(2,1)}), bf16[64,24,768]{2,1,0:T(8,128)(2,1)S(1)}, u32[]{:S(2)}, u32[]{:S(2)}) async-start(bf16[64,24,768]{2,1,0:T(8,128)(2,1)} %bitcast.80), calls=%async_computation | async-start | bytes 4718592 | tf_op jit(solution)/shard_map/all_to_all | solution.py:74
  28.1 249.5 %all-gather.6.cloned.1.call-start = ((), (), s32[]{:S(2)}) async-start(), calls=%async_computation.5 | async-start | bytes 7864320 | tf_op jit(solution)/shard_map/all_gather | solution.py:48
  28.2 5.4 %copy-start.3 = (bf16[128,4096]{1,0:T(8,128)(2,1)S(1)}, bf16[128,4096]{1,0:T(8,128)(2,1)}, u32[]{:S(2)}) copy-start(bf16[128,4096]{1,0:T(8,128)(2,1)} %param.6) | copy-start | bytes 3145732
  84.9 176.7 %copy-start.4 = (bf16[2,4096,16]{1,2,0:T(8,128)(2,1)S(1)}, bf16[2,4096,16]{1,2,0:T(8,128)(2,1)}, u32[]{:S(2)}) copy-start(bf16[2,4096,16]{1,2,0:T(8,128)(2,1)} %param.10) | copy-start | bytes 786436
  84.9 180.2 %all-to-all-start.1 = ((bf16[64,24,2048]{2,1,0:T(8,128)(2,1)}), bf16[64,24,2048]{2,1,0:T(8,128)(2,1)}, u32[]{:S(2)}, u32[]{:S(2)}) async-start(bf16[64,24,2048]{2,1,0:T(8,128)(2,1)} %bitcast.79), calls=%async_computation.1 | async-start | bytes 12582912 | tf_op jit(solution)/shard_map/all_to_all | solution.py:62
  90.7 239.4 %all-gather.4.cloned.1.call-start = ((), (), s32[]{:S(2)}) async-start(), calls=%async_computation.4 | async-start | bytes 7864320 | tf_op jit(solution)/shard_map/all_gather | solution.py:50
  90.8 170.7 %collective-permute-start = (bf16[512,1536]{1,0:T(8,128)(2,1)}, bf16[512,1536]{1,0:T(8,128)(2,1)}, u32[]{:S(2)}, u32[]{:S(2)}) collective-permute-start(bf16[512,1536]{1,0:T(8,128)(2,1)} %get-tuple-element.4), channel_id=1, source_target_pairs={{0,4},{4,0},{1,5},{5,1},{2,6},{6,2},{3,7},{7,3},{8,12},{12,8},{9,1... | collective-permute-start | bytes 4718600 | tf_op jit(solution)/shard_map/ppermute | solution.py:49
  267.4 3.0 copy-start.5
  270.4 3.3 copy-start.1
  273.8 1.0 copy-start.7
  330.1 13.2 %copy-start.2 = (bf16[512,2048]{1,0:T(8,128)(2,1)S(1)}, bf16[512,2048]{1,0:T(8,128)(2,1)}, u32[]{:S(2)}) copy-start(bf16[512,2048]{1,0:T(8,128)(2,1)} %copy-done.1) | copy-start | bytes 6291460
  330.1 13.2 %copy-start.6 = (bf16[256,2048]{1,0:T(8,128)(2,1)S(1)}, bf16[256,2048]{1,0:T(8,128)(2,1)}, u32[]{:S(2)}) copy-start(bf16[256,2048]{1,0:T(8,128)(2,1)} %copy-done.5) | copy-start | bytes 3145732
  342.6 1.3 copy-start.8
Sparse Core Ops, SparseCore 0:
  32.3 69.2 all-gather.5
  261.6 68.4 all-gather.3
where the time goes:
time: 376 us
  waiting for transfers between devices  259 us (69%)
  matrix products  43.6 us (12%)
  blocking collectives  22.1 us (6%)
  starting transfers between devices  19.7 us (5%)
  between operations  14.3 us (4%)
  local copies, waits for them, and re-layouts  11.2 us (3%)
  other arithmetic  6.15 us (2%)
    ppermute x1, waiting for transfers between devices, local(): got = lax.ppermute(other, 'zl', [(0, 1), (1, 0)])  169 us
    all_to_all x1, waiting for transfers between devices, local(): lax.all_to_all(send_g, PLANE, split_axis=0, concat_axis=0, tiled=True)  46.8 us
    dot_general x15, matrix products, dot(): lax.dot_general(a, b, (dims, ((), ())), preferred_element_type=jnp.float32)  43.6 us
    all_gather x1, waiting for transfers between devices, local(): weight_far = lax.all_gather(got, 'x', axis=0, tiled=True)  42.7 us
    all_to_all x1, starting transfers between devices, local(): lax.all_to_all(send_g, PLANE, split_axis=0, concat_axis=0, tiled=True)  12.1 us
    all_to_all x1, blocking collectives, local(): lax.all_to_all(total, DP_AXES, split_axis=0, concat_axis=0, tiled=True)  11.1 us
    all_to_all x1, blocking collectives, local(): parts = lax.all_to_all(parts, 'x', split_axis=0, concat_axis=0, tiled=True)  11 us
  transfers between devices with their start and end apart: 5, of which 3 were waited for; matrix products, arithmetic and copies ran while one was open for 9% of the time, Pallas kernels for 0%

commit v1 on v0

--- a/solution.py
+++ b/solution.py
@@ -7,6 +7,13 @@
 EXPERT_AXES = ("zh", "y", "c")
 DP_AXES = ("zl", "x")
 PLANE = ("zh", "y", "c", "zl")
+
+
+def all_by_exchange(x, axis, dim):
+    devices = lax.axis_size(axis)
+    blocks = jnp.stack([x for _ in range(devices)])
+    blocks = lax.all_to_all(blocks, axis, split_axis=0, concat_axis=0)
+    return jnp.concatenate(blocks, axis=dim)
 
 
 def dot(a, b, dims=((1,), (0,))):
@@ -47,7 +54,7 @@
     other = lax.dynamic_index_in_dim(frozen_gate_weight, 1 - zl, 0, keepdims=False)
     weight_near = lax.all_gather(mine, "x", axis=0, tiled=True)
     got = lax.ppermute(other, "zl", [(0, 1), (1, 0)])
-    weight_far = lax.all_gather(got, "x", axis=0, tiled=True)
+    weight_far = all_by_exchange(got, "x", 0)
     first = lax.dynamic_index_in_dim(adapter_first, zl, 0, keepdims=False)
     second = lax.dynamic_index_in_dim(adapter_second, zl, 0, keepdims=False)
     half_width = width // 2

time: 376 us -> 387 us (1.029)
  starting transfers between devices: 19.7 us -> 25 us
  local copies, waits for them, and re-layouts: 11.2 us -> 15.4 us
    all_to_all x0 -> x1, waiting for transfers between devices: none -> 46.1 us  [all_by_exchange(): blocks = lax.all_to_all(blocks, axis, split_axis=0, concat_axis=0)]
    all_gather x1 -> x0, waiting for transfers between devices: 42.7 us -> none  [local(): weight_far = lax.all_gather(got, 'x', axis=0, tiled=True)]
    all_to_all x0 -> x1, starting transfers between devices: none -> 5.54 us  [all_by_exchange(): blocks = lax.all_to_all(blocks, axis, split_axis=0, concat_axis=0)]
    another operation x0 -> x1, local copies, waits for them, and re-layouts: none -> 4.48 us  [all_by_exchange(): blocks = jnp.stack([x for _ in range(devices)])]
    all_to_all x1, waiting for transfers between devices: 46.8 us -> 50.8 us  [local(): lax.all_to_all(send_g, PLANE, split_axis=0, concat_axis=0, tiled=True)]
  transfers between devices with their start and end apart: 5 -> 5, of which waited for: 3 -> 3; matrix products, arithmetic and copies ran while one was open for 9% -> 10% of each run, Pallas kernels for 0% -> 0%
where the time goes in v1:
time: 387 us; the launch traced here: 386 us
  waiting for transfers between devices  262 us (68%)
  matrix products  43 us (11%)
  starting transfers between devices  25 us (6%)
  blocking collectives  19.8 us (5%)
  local copies, waits for them, and re-layouts  15.4 us (4%)
  between operations  14.3 us (4%)
  other arithmetic  6.15 us (2%)
    ppermute x1, waiting for transfers between devices, local(): got = lax.ppermute(other, 'zl', [(0, 1), (1, 0)])  165 us
    all_to_all x1, waiting for transfers between devices, local(): lax.all_to_all(send_g, PLANE, split_axis=0, concat_axis=0, tiled=True)  50.8 us
    all_to_all x1, waiting for transfers between devices, all_by_exchange(): blocks = lax.all_to_all(blocks, axis, split_axis=0, concat_axis=0)  46.1 us
    dot_general x15, matrix products, dot(): lax.dot_general(a, b, (dims, ((), ())), preferred_element_type=jnp.float32)  43 us
    all_to_all x1, starting transfers between devices, local(): lax.all_to_all(send_g, PLANE, split_axis=0, concat_axis=0, tiled=True)  12.2 us
    all_to_all x1, blocking collectives, local(): lax.all_to_all(total, DP_AXES, split_axis=0, concat_axis=0, tiled=True)  10.2 us
    all_to_all x1, blocking collectives, local(): parts = lax.all_to_all(parts, 'x', split_axis=0, concat_axis=0, tiled=True)  9.59 us
  transfers between devices with their start and end apart: 5, of which 3 were waited for; matrix products, arithmetic and copies ran while one was open for 10% of the time, Pallas kernels for 0%

profile of v1, /device:TPU:8, one launch (start us, length us, event | category | flops | bytes accessed | tf_op | source)
XLA Modules:
  0.0 386.0 jit_solution(11924985710725054050)
XLA Ops:
  7.2 0.9 convert_reduce_fusion
  8.2 0.7 multiply_add_fusion
  8.9 2.7 fusion.96
  11.7 1.4 compare_and_fusion.1
  13.1 2.8 convolution_convert_fusion.1
  15.9 12.2 %all-to-all-start = ((bf16[64,24,768]{2,1,0:T(8,128)(2,1)}), bf16[64,24,768]{2,1,0:T(8,128)(2,1)S(1)}, u32[]{:S(2)}, u32[]{:S(2)}) async-start(bf16[64,24,768]{2,1,0:T(8,128)(2,1)} %bitcast.81), calls=%async_computation | async-start | bytes 4718592 | tf_op jit(solution)/shard_map/all_to_all | solution.py:81
  28.2 1.4 fusion.23
  29.7 4.4 %convolution_convert_fusion = bf16[1536,2048]{1,0:T(8,128)(2,1)} fusion(pred[1536,128]{1,0:T(32,128)(4,1)S(1)} %get-tuple-element.23, pred[1536,128]{1,0:T(32,128)(4,1)S(1)} %get-tuple-element.22, bf16[128,2048]{1,0:T(8,128)(2,1)S(1)} %get-tuple-element.9, bf16[128,2048]{1,0:T(8,128)(2,1)S(1)} %get-tuple-element.8), kind=kOutput, calls=%fused_computation | convolution fusion | flops 1616248832 | bytes 7733248 | tf_op jit(solution)/shard_map/dot_general | solution.py:20
  34.1 50.8 %all-to-all-done = bf16[64,24,768]{2,1,0:T(8,128)(2,1)S(1)} async-done(((bf16[64,24,768]{2,1,0:T(8,128)(2,1)}), bf16[64,24,768]{2,1,0:T(8,128)(2,1)S(1)}, u32[]{:S(2)}, u32[]{:S(2)}) %all-to-all-start) | async-done | bytes 2359328 | tf_op jit(solution)/shard_map/all_to_all | solution.py:81
  84.9 5.7 %all-to-all-start.1 = ((bf16[64,24,2048]{2,1,0:T(8,128)(2,1)}), bf16[64,24,2048]{2,1,0:T(8,128)(2,1)}, u32[]{:S(2)}, u32[]{:S(2)}) async-start(bf16[64,24,2048]{2,1,0:T(8,128)(2,1)} %bitcast.80), calls=%async_computation.1 | async-start | bytes 12582912 | tf_op jit(solution)/shard_map/all_to_all | solution.py:69
  90.7 3.8 dynamic-slice_bitcast_fusion
  94.5 1.6 collective-permute-start
  96.1 165.3 %collective-permute-done = bf16[512,1536]{1,0:T(8,128)(2,1)} collective-permute-done((bf16[512,1536]{1,0:T(8,128)(2,1)}, bf16[512,1536]{1,0:T(8,128)(2,1)}, u32[]{:S(2)}, u32[]{:S(2)}) %collective-permute-start) | collective-permute-done | bytes 1572896 | tf_op jit(solution)/shard_map/ppermute | solution.py:56
  261.4 4.5 %stack.16 = bf16[4,512,1536]{2,1,0:T(8,128)(2,1)} broadcast(bf16[512,1536]{1,0:T(8,128)(2,1)} %collective-permute-done), dimensions={1,2} | broadcast | bytes 7864320 | tf_op jit(solution)/shard_map/stack | solution.py:14
  265.9 5.5 %all-to-all-start.2 = ((bf16[4,512,1536]{2,1,0:T(8,128)(2,1)}), bf16[4,512,1536]{2,1,0:T(8,128)(2,1)}, u32[]{:S(2)}, u32[]{:S(2)}) async-start(bf16[4,512,1536]{2,1,0:T(8,128)(2,1)} %stack.16), calls=%async_computation.2 | async-start | bytes 12582912 | tf_op jit(solution)/shard_map/all_to_all | solution.py:15
  271.5 1.2 convolution_convert_fusion.4
  272.7 1.2 convolution_convert_fusion.5
  273.9 1.0 slice_bitcast_fusion.7
  274.9 2.4 convolution_convert_fusion.3
  277.3 3.0 slice_bitcast_fusion
  280.3 0.9 fusion.14
  281.2 2.4 convolution_convert_fusion.2
  283.6 0.9 fusion.8
  284.6 3.0 fusion.44
  287.6 8.9 %fusion = f32[768,1536]{1,0:T(8,128)} fusion(bf16[1,2048,1536]{2,1,0:T(8,128)(2,1)} %all-gather.3.cloned.1.call-done, bf16[256,2048]{1,0:T(8,128)(2,1)} %copy-done.5, bf16[512,2048]{1,0:T(8,128)(2,1)S(1)} %get-tuple-element.3), kind=kOutput, calls=%fused_computation.1 | convolution fusion | flops 4838129664 | bytes 14155776 | tf_op jit(solution)/shard_map/dot_general | solution.py:20
  296.5 46.1 %all-to-all-done.2 = bf16[4,512,1536]{2,1,0:T(8,128)(2,1)} async-done(((bf16[4,512,1536]{2,1,0:T(8,128)(2,1)}), bf16[4,512,1536]{2,1,0:T(8,128)(2,1)}, u32[]{:S(2)}, u32[]{:S(2)}) %all-to-all-start.2) | async-done | bytes 6291488 | tf_op jit(solution)/shard_map/all_to_all | solution.py:15
  342.6 12.8 %multiply_convert_fusion = bf16[768,1536]{1,0:T(8,128)(2,1)S(1)} fusion(f32[768,1536]{1,0:T(8,128)} %fusion.44, f32[768,1536]{1,0:T(8,128)} %fusion, bf16[2048,1536]{1,0:T(8,128)(2,1)} %bitcast.17, bf16[256,768]{1,0:T(8,128)(2,1)} %convolution_convert_fusion.4, bf16[512,768]{1,0:T(8,128)(2,1)} %get-tuple-element.7, ...), kind=kOutput, calls=%fused_computation.3 | convolution fusion | flops 4861722624 | bytes 23592960 | tf_op jit(solution)/shard_map/dot_general | solution.py:20
  355.3 0.7 convolution_convert_fusion.6
  357.6 9.6 %all_to_all.25 = f32[4,16,1408]{2,1,0:T(8,128)S(1)} all-to-all(f32[4,16,1408]{2,1,0:T(8,128)S(1)} %bitcast.85), channel_id=1, replica_groups=mesh['zh'=4,'y'=4,'c'=2,'zl'=2,'x'=4] {'x'}, dimensions={0} | all-to-all | bytes 720896 | tf_op jit(solution)/shard_map/all_to_all | solution.py:112
  367.3 10.2 %all_to_all.26 = bf16[8,16,1408]{2,1,0:T(8,128)(2,1)S(1)} all-to-all(bf16[8,16,1408]{2,1,0:T(8,128)(2,1)S(1)} %broadcast_in_dim.2), channel_id=1, replica_groups=mesh['zh'=4,'y'=4,'c'=2,'zl'=2,'x'=4] {'zl','x'}, dimensions={0} | all-to-all | bytes 720896 | tf_op jit(solution)/shard_map/all_to_all | solution.py:115
  377.5 0.7 slice_convert_fusion
  378.3 0.8 convert_bitcast_fusion
  (45 shorter events, 2.1 us)
Async XLA Ops:
  7.2 277.4 %copy-start = (bf16[2,16,1536]{2,1,0:T(8,128)(2,1)S(1)}, bf16[2,16,1536]{2,1,0:T(8,128)(2,1)}, u32[]{:S(2)}) copy-start(bf16[2,16,1536]{2,1,0:T(8,128)(2,1)} %param.11) | copy-start | bytes 294916
  15.9 13.7 %copy-start.3 = (bf16[128,4096]{1,0:T(8,128)(2,1)S(1)}, bf16[128,4096]{1,0:T(8,128)(2,1)}, u32[]{:S(2)}) copy-start(bf16[128,4096]{1,0:T(8,128)(2,1)} %param.6) | copy-start | bytes 3145732
  15.9 69.0 %all-to-all-start = ((bf16[64,24,768]{2,1,0:T(8,128)(2,1)}), bf16[64,24,768]{2,1,0:T(8,128)(2,1)S(1)}, u32[]{:S(2)}, u32[]{:S(2)}) async-start(bf16[64,24,768]{2,1,0:T(8,128)(2,1)} %bitcast.81), calls=%async_computation | async-start | bytes 4718592 | tf_op jit(solution)/shard_map/all_to_all | solution.py:81
  84.9 176.5 %all-to-all-start.1 = ((bf16[64,24,2048]{2,1,0:T(8,128)(2,1)}), bf16[64,24,2048]{2,1,0:T(8,128)(2,1)}, u32[]{:S(2)}, u32[]{:S(2)}) async-start(bf16[64,24,2048]{2,1,0:T(8,128)(2,1)} %bitcast.80), calls=%async_computation.1 | async-start | bytes 12582912 | tf_op jit(solution)/shard_map/all_to_all | solution.py:69
  90.6 197.0 %all-gather.3.cloned.1.call-start = ((), (), s32[]{:S(2)}) async-start(), calls=%async_computation.5 | async-start | bytes 7864320 | tf_op jit(solution)/shard_map/all_gather | solution.py:55
  94.5 166.9 %collective-permute-start = (bf16[512,1536]{1,0:T(8,128)(2,1)}, bf16[512,1536]{1,0:T(8,128)(2,1)}, u32[]{:S(2)}, u32[]{:S(2)}) collective-permute-start(bf16[512,1536]{1,0:T(8,128)(2,1)} %get-tuple-element.4), channel_id=1, source_target_pairs={{0,4},{4,0},{1,5},{5,1},{2,6},{6,2},{3,7},{7,3},{8,12},{12,8},{9,1... | collective-permute-start | bytes 4718600 | tf_op jit(solution)/shard_map/ppermute | solution.py:56
  265.9 5.6 %copy-start.4 = (bf16[2,4096,16]{1,2,0:T(8,128)(2,1)S(1)}, bf16[2,4096,16]{1,2,0:T(8,128)(2,1)}, u32[]{:S(2)}) copy-start(bf16[2,4096,16]{1,2,0:T(8,128)(2,1)} %param.10) | copy-start | bytes 786436
  265.9 76.7 %all-to-all-start.2 = ((bf16[4,512,1536]{2,1,0:T(8,128)(2,1)}), bf16[4,512,1536]{2,1,0:T(8,128)(2,1)}, u32[]{:S(2)}, u32[]{:S(2)}) async-start(bf16[4,512,1536]{2,1,0:T(8,128)(2,1)} %stack.16), calls=%async_computation.2 | async-start | bytes 12582912 | tf_op jit(solution)/shard_map/all_to_all | solution.py:15
  277.3 3.0 copy-start.5
  280.3 3.3 copy-start.1
  283.6 1.0 copy-start.7
  342.6 13.5 %copy-start.2 = (bf16[512,2048]{1,0:T(8,128)(2,1)S(1)}, bf16[512,2048]{1,0:T(8,128)(2,1)}, u32[]{:S(2)}) copy-start(bf16[512,2048]{1,0:T(8,128)(2,1)} %copy-done.1) | copy-start | bytes 6291460
  342.6 13.5 %copy-start.8 = (bf16[256,2048]{1,0:T(8,128)(2,1)S(1)}, bf16[256,2048]{1,0:T(8,128)(2,1)}, u32[]{:S(2)}) copy-start(bf16[256,2048]{1,0:T(8,128)(2,1)} %copy-done.7) | copy-start | bytes 3145732
  355.3 1.3 copy-start.6
Sparse Core Ops, SparseCore 0:
  94.7 69.2 all-gather.2
